TPU v7x, 32 devices: a whole 2x2x4 slice. The times are simulated.
32 devices in a mesh: row: 2 (over x), col: 16 (over z, y, core).
Axes of the slice: x: 2, y: 2, z: 4, core: 2. Of those that a mesh axis runs over, the one named last changes fastest.
Arguments:
- matrix: bfloat16 [1024, 65536], P('row', 'col'), may hold values from -0.1875 to 0.1875
- measured: float32 [256, 1024], P(None, 'row'), may hold values from -160 to 160
- support: int32 [4, 1024], replicated, may hold values from 0 to 65535, as said below
Outputs:
- estimate: float32 [256, 65536], P('row', 'col')
- row_norms: float32 [65536], P('col')
- residual_energy: float32 [4], replicated
Inputs may be any that keep to these rules, and one draw needn't show every extreme that they name: Each row of support lists 1024 distinct signal-row indices in increasing order; in every row, each aligned block of 4096 indices (the signal rows of one index of col) holds at most 128 of them, and some block exactly 128.
All inputs are finite; a program needn't handle non-finite values.
Results may differ from a plain program's by a relative error of at most 0.015.
Values may be sent and summed in bfloat16 or wider, within the bound.
A program may use at most 64 MiB of HBM per device.

v0:
```python
import jax
import jax.numpy as jnp
from jax import lax
from jax.sharding import PartitionSpec as P

KMAX = 128
STEP_SIZE = 0.25
HI = lax.Precision.HIGHEST
NT = (((1,), (1,)), ((), ()))


def window(support_row, start, width):
    below = jnp.sum((support_row < start).astype(jnp.int32))
    local = support_row - start
    inside = (local >= 0) & (local < width)
    slot = jnp.arange(support_row.shape[0]) - below
    chosen = (slot[None, :] == jnp.arange(KMAX)[:, None]) & inside[None, :]
    return jnp.sum(jnp.where(chosen, local[None, :] + 1, 0), axis=1) - 1


def local(matrix, measured, support):
    signals = measured.shape[0]
    n_row = lax.axis_size("row")
    rows_mine = signals // n_row
    columns = matrix.shape[1]
    offset = lax.axis_index("col") * columns
    iterations = support.shape[0]
    total_count = signals * measured.shape[1] * n_row
    lanes = jnp.arange(columns)
    index = [window(support[t], offset, columns) for t in range(iterations)]
    onehot = [(i[:, None] == lanes[None, :]).astype(jnp.bfloat16) for i in index]
    kept = [
        lax.dot_general(e, matrix, NT, preferred_element_type=jnp.float32).astype(jnp.bfloat16)
        for e in onehot[:-1]
    ]
    residual = measured
    current = jnp.zeros((signals, KMAX), jnp.float32)
    energies = []
    for t in range(iterations):
        energies.append(jnp.sum(residual * residual))
        half = residual.astype(jnp.bfloat16)
        if t == iterations - 1:
            break
        part = lax.dot_general(half, kept[t], NT, preferred_element_type=jnp.float32)
        gradient = lax.psum(part.astype(jnp.bfloat16), "row").astype(jnp.float32)
        if t:
            same = (index[t - 1][:, None] == index[t][None, :]) & (index[t] >= 0)[None, :]
            current = jnp.dot(current, same.astype(jnp.float32), precision=HI)
        current = current + STEP_SIZE * gradient
        image = jnp.dot(current.astype(jnp.bfloat16), kept[t], preferred_element_type=jnp.float32)
        residual = measured - lax.psum(image.astype(jnp.bfloat16), "col").astype(jnp.float32)
    gradient = lax.psum_scatter(
        jnp.dot(half, matrix, preferred_element_type=jnp.float32).astype(jnp.bfloat16),
        "row",
        scatter_dimension=0,
        tiled=True,
    ).astype(jnp.float32)
    mine = lax.dynamic_slice_in_dim(current, lax.axis_index("row") * rows_mine, rows_mine, 0)
    stepped = jnp.dot(mine, onehot[-2].astype(jnp.float32), precision=HI) + STEP_SIZE * gradient
    keep = jnp.sum(onehot[-1].astype(jnp.float32), axis=0)
    sums = jnp.concatenate([jnp.sum(stepped * stepped, axis=0), jnp.stack(energies)])
    sums = lax.psum(sums, "row")
    return (stepped * keep[None, :], jnp.sqrt(sums[:columns]), sums[columns:] / total_count)


def solution(mesh):
    placed = (P("row", "col"), P(None, "row"), P())
    return jax.shard_map(
        local,
        mesh=mesh,
        in_specs=placed,
        out_specs=(P("row", "col"), P("col"), P()),
        check_vma=False,
    )
```

profile of v0, /device:TPU:0, one launch (start us, length us, event | category | flops | bytes accessed | tf_op | source)
XLA Modules:
  0.0 428.1 jit_solution(17295335813921915850)
XLA Ops:
  7.2 0.0 all-reduce.7.cloned.1.call-start
  7.2 0.9 and_reduce_fusion
  8.2 1.6 subtract_add_fusion
  9.8 1.3 iota_subtract_fusion.2
  11.1 0.2 select_reduce_fusion.3
  11.3 0.0 copy-start
  11.3 3.8 fusion.5
  15.0 0.0 copy-done
  15.0 0.9 fusion.7
  15.9 0.0 all-reduce.7.cloned.1.call-update
  15.9 0.0 all-reduce.9.cloned.1.call-start
  16.0 0.2 select_reduce_fusion.2
  16.2 3.7 fusion.4
  19.9 19.9 %all-reduce.7.cloned.1.call-done = bf16[256,128]{0,1:T(8,128)(2,1)} async-done(((bf16[256,128]{0,1:T(8,128)(2,1)}), bf16[256,128]{0,1:T(8,128)(2,1)}) %all-reduce.7.cloned.1.call-update) | async-done | bytes 65552 | tf_op jit(solution)/shard_map/psum | solution.py:45
  39.8 1.8 convolution_convert_fusion.3
  41.5 0.0 all-reduce.9.cloned.1.call-update
  41.6 0.0 all-reduce.11.cloned.1.call-start
  41.6 1.3 iota_subtract_fusion
  42.9 0.2 select_reduce_fusion.1
  43.1 90.4 %all-reduce.9.cloned.1.call-done = bf16[256,512]{1,0:T(8,128)(2,1)} async-done(((bf16[256,512]{1,0:T(8,128)(2,1)}), bf16[256,512]{1,0:T(8,128)(2,1)}) %all-reduce.9.cloned.1.call-update) | async-done | bytes 262160 | tf_op jit(solution)/shard_map/psum | solution.py:51
  133.4 1.8 convolution_convert_fusion.5
  135.2 0.0 all-reduce.11.cloned.1.call-update
  135.3 0.0 all-reduce.13.cloned.1.call-start
  135.3 22.4 %all-reduce.11.cloned.1.call-done = bf16[256,128]{0,1:T(8,128)(2,1)} async-done(((bf16[256,128]{0,1:T(8,128)(2,1)}), bf16[256,128]{0,1:T(8,128)(2,1)}) %all-reduce.11.cloned.1.call-update) | async-done | bytes 65552 | tf_op jit(solution)/shard_map/psum | solution.py:45
  157.7 1.2 convolution_add_fusion.2
  158.9 1.0 convolution_convert_fusion.2
  159.9 0.0 all-reduce.13.cloned.1.call-update
  159.9 0.0 all-reduce.15.cloned.1.call-start
  160.0 3.7 fusion.6
  163.7 87.6 %all-reduce.13.cloned.1.call-done = bf16[256,512]{1,0:T(8,128)(2,1)} async-done(((bf16[256,512]{1,0:T(8,128)(2,1)}), bf16[256,512]{1,0:T(8,128)(2,1)}) %all-reduce.13.cloned.1.call-update) | async-done | bytes 262160 | tf_op jit(solution)/shard_map/psum | solution.py:51
  251.3 1.8 convolution_convert_fusion.4
  253.1 0.0 all-reduce.15.cloned.1.call-update
  253.1 0.0 all-reduce.17.cloned.1.call-start
  253.2 22.2 %all-reduce.15.cloned.1.call-done = bf16[256,128]{0,1:T(8,128)(2,1)} async-done(((bf16[256,128]{0,1:T(8,128)(2,1)}), bf16[256,128]{0,1:T(8,128)(2,1)}) %all-reduce.15.cloned.1.call-update) | async-done | bytes 65552 | tf_op jit(solution)/shard_map/psum | solution.py:45
  275.4 1.2 convolution_add_fusion.1
  276.6 1.0 convolution_convert_fusion.1
  277.5 0.0 all-reduce.17.cloned.1.call-update
  277.5 0.0 reduce-scatter.2.cloned.1.call-start
  277.6 91.3 %all-reduce.17.cloned.1.call-done = bf16[256,512]{1,0:T(8,128)(2,1)} async-done(((bf16[256,512]{1,0:T(8,128)(2,1)}), bf16[256,512]{1,0:T(8,128)(2,1)}) %all-reduce.17.cloned.1.call-update) | async-done | bytes 262160 | tf_op jit(solution)/shard_map/psum | solution.py:51
  368.9 4.9 %convolution_convert_fusion = bf16[256,4096]{1,0:T(8,128)(2,1)} fusion(bf16[512,4096]{1,0:T(8,128)(2,1)} %param.3, f32[256,512]{1,0:T(8,128)S(1)} %copy-done, bf16[256,512]{1,0:T(8,128)(2,1)} %all-reduce.17.cloned.1.call-done), kind=kOutput, calls=%fused_computation | convolution fusion | flops 1075183616 | bytes 7077888 | tf_op jit(solution)/shard_map/dot_general | solution.py:53
  373.8 0.0 copy-start.1
  373.8 0.0 copy-start.2
  373.8 0.0 copy-start.3
  373.8 0.0 reduce-scatter.2.cloned.1.call-update
  373.8 0.2 select_reduce_fusion
  374.0 0.3 convert_reduce_fusion
  374.3 0.4 copy-done.1
  374.7 0.1 copy-done.2
  374.8 0.1 copy-done.3
  374.9 0.9 multiply_reduce_fusion.1
  375.8 30.5 %reduce-scatter.2.cloned.1.call-done = bf16[128,4096]{1,0:T(8,128)(2,1)} async-done(((bf16[256,4096]{1,0:T(8,128)(2,1)}), bf16[128,4096]{1,0:T(8,128)(2,1)}) %reduce-scatter.2.cloned.1.call-update) | async-done | bytes 1048592 | tf_op jit(solution)/shard_map/reduce_scatter | solution.py:52
  406.4 4.1 multiply_reduce_fusion
  410.4 2.6 concatenate.3
  413.1 7.1 %psum.55 = f32[4100]{0:T(1024)S(1)} all-reduce(f32[4100]{0:T(1024)S(1)} %concatenate.3), channel_id=1, replica_groups=mesh['row'=2,'col'=16] {'row'}, use_global_device_ids=true, to_apply=%region_21.22 | all-reduce | flops 4100 | bytes 32800 | tf_op jit(solution)/shard_map/psum | solution.py:62
  420.2 0.5 slice_multiply_fusion
  420.7 0.6 slice_sqrt_fusion
  (6 shorter events, 0.0 us)
Async XLA Ops:
  7.2 32.6 %all-reduce.7.cloned.1.call-start = ((), (), s32[]{:S(2)}) async-start(), calls=%async_computation.1 | async-start | bytes 131072 | tf_op jit(solution)/shard_map/psum | solution.py:45
  11.3 3.8 copy-start
  15.9 117.5 %all-reduce.9.cloned.1.call-start = ((), (), s32[]{:S(2)}) async-start(), calls=%async_computation.2 | async-start | bytes 524288 | tf_op jit(solution)/shard_map/psum | solution.py:51
  41.6 116.1 %all-reduce.11.cloned.1.call-start = ((), (), s32[]{:S(2)}) async-start(), calls=%async_computation.3 | async-start | bytes 131072 | tf_op jit(solution)/shard_map/psum | solution.py:45
  135.3 116.0 %all-reduce.13.cloned.1.call-start = ((), (), s32[]{:S(2)}) async-start(), calls=%async_computation.4 | async-start | bytes 524288 | tf_op jit(solution)/shard_map/psum | solution.py:51
  159.9 115.5 %all-reduce.15.cloned.1.call-start = ((), (), s32[]{:S(2)}) async-start(), calls=%async_computation.5 | async-start | bytes 131072 | tf_op jit(solution)/shard_map/psum | solution.py:45
  253.1 115.8 %all-reduce.17.cloned.1.call-start = ((), (), s32[]{:S(2)}) async-start(), calls=%async_computation.6 | async-start | bytes 524288 | tf_op jit(solution)/shard_map/psum | solution.py:51
  277.5 128.8 %reduce-scatter.2.cloned.1.call-start = ((), (), s32[]{:S(2)}) async-start(), calls=%async_computation.7 | async-start | bytes 3145728 | tf_op jit(solution)/shard_map/reduce_scatter | solution.py:52
  373.8 0.9 copy-start.1
  373.8 1.0 copy-start.2
  373.8 1.1 copy-start.3
Sparse Core Ops, SparseCore 0:
  16.0 23.6 all-reduce.6
  43.7 89.6 all-reduce.8
  136.3 21.4 all-reduce.10
  161.5 89.6 all-reduce.12
  253.9 21.4 all-reduce.14
  279.2 89.6 all-reduce.16
  373.9 32.3 reduce-scatter.1
where the time goes:
time: 429 us; the launch traced here: 428 us
  waiting for transfers between devices  364 us (85%)
  matrix products  30.6 us (7%)
  between operations  14.2 us (3%)
  other arithmetic  7.66 us (2%)
  blocking collectives  7.1 us (2%)
    psum x3, waiting for transfers between devices, local(): lax.psum(image.astype(jnp.bfloat16), 'col').astype(jnp.float32)  269 us
    psum x3, waiting for transfers between devices, local(): gradient = lax.psum(part.astype(jnp.bfloat16), 'row').astype(jnp.float32)  64.5 us
    reduce_scatter x1, waiting for transfers between devices, local(): lax.psum_scatter(jnp.dot(half, matrix, preferred_element_type=jnp.float32...  30.5 us
    dot_general x3, matrix products, local(): lax.dot_general(e, matrix, NT, preferred_element_type=jnp.float32)  11.1 us
  transfers between devices with their start and end apart: 7, of which 7 were waited for; matrix products, arithmetic and copies ran while one was open for 2% of the time, Pallas kernels for 0%

commit v1 on v0

--- a/solution.py
+++ b/solution.py
@@ -42,7 +42,9 @@
         if t == iterations - 1:
             break
         part = lax.dot_general(half, kept[t], NT, preferred_element_type=jnp.float32)
-        gradient = lax.psum(part.astype(jnp.bfloat16), "row").astype(jnp.float32)
+        gradient = jnp.sum(lax.all_gather(part.astype(jnp.bfloat16), "row"), axis=0).astype(
+            jnp.float32
+        )
         if t:
             same = (index[t - 1][:, None] == index[t][None, :]) & (index[t] >= 0)[None, :]
             current = jnp.dot(current, same.astype(jnp.float32), precision=HI)

time: 429 us -> 369 us (0.86)
  waiting for transfers between devices: 364 us -> 295 us
  blocking collectives: 7.1 us -> 23.2 us
  matrix products: 30.6 us -> 23.9 us
    psum x3 -> x0, waiting for transfers between devices: 64.5 us -> none  [local(): gradient = lax.psum(part.astype(jnp.bfloat16), 'row').astype(jnp.float32)]
    all_gather x0 -> x3, blocking collectives: none -> 16.1 us  [local(): lax.all_gather(part.astype(jnp.bfloat16), 'row')]
    psum x3, waiting for transfers between devices: 269 us -> 265 us  [local(): lax.psum(image.astype(jnp.bfloat16), 'col').astype(jnp.float32)]
  transfers between devices with their start and end apart: 7 -> 4, of which waited for: 7 -> 4; matrix products, arithmetic and copies ran while one was open for 2% -> 2% of each run, Pallas kernels for 0% -> 0%
where the time goes in v1:
time: 369 us
  waiting for transfers between devices  295 us (80%)
  matrix products  23.9 us (6%)
  blocking collectives  23.2 us (6%)
  between operations  13.9 us (4%)
  other arithmetic  8.19 us (2%)
  local copies, waits for them, and re-layouts  3.96 us (1%)
    psum x3, waiting for transfers between devices, local(): lax.psum(image.astype(jnp.bfloat16), 'col').astype(jnp.float32)  265 us
    reduce_scatter x1, waiting for transfers between devices, local(): lax.psum_scatter(jnp.dot(half, matrix, preferred_element_type=jnp.float32...  30.5 us
    all_gather x3, blocking collectives, local(): lax.all_gather(part.astype(jnp.bfloat16), 'row')  16.1 us
    dot_general x3, matrix products, local(): lax.dot_general(e, matrix, NT, preferred_element_type=jnp.float32)  9.09 us
  transfers between devices with their start and end apart: 4, of which 4 were waited for; matrix products, arithmetic and copies ran while one was open for 2% of the time, Pallas kernels for 0%

profile of v1, /device:TPU:0, one launch (start us, length us, event | category | flops | bytes accessed | tf_op | source)
XLA Modules:
  0.0 368.8 jit_solution(1508874714919351130)
XLA Ops:
  7.2 0.0 all-reduce.4.cloned.1.call-start
  7.2 0.9 and_reduce_fusion
  8.2 1.7 subtract_add_fusion
  9.8 1.3 iota_subtract_fusion.2
  11.1 0.2 select_reduce_fusion.3
  11.3 0.0 copy-start
  11.3 3.8 %fusion.5 = bf16[128,512]{1,0:T(8,128)(2,1)S(1)} fusion(bf16[512,4096]{1,0:T(8,128)(2,1)} %param.3, s32[128]{0:T(128)S(1)} %broadcast_add_fusion.3), kind=kOutput, calls=%fused_computation.16 | convolution fusion | flops 537460736 | bytes 4325888 | tf_op jit(solution)/shard_map/dot_general | solution.py:33
  15.1 0.0 copy-done
  15.1 0.2 fusion.7
  15.3 5.9 %all-gather = bf16[512,128]{0,1:T(8,128)(2,1)S(1)} all-gather(bf16[256,128]{0,1:T(8,128)(2,1)S(1)} %fusion.7), channel_id=2, replica_groups=mesh['row'=2,'col'=16] {'row'}, dimensions={0}, use_global_device_ids=true | all-gather | bytes 196608 | tf_op jit(solution)/shard_map/all_gather | solution.py:45
  21.2 0.3 reduce_sum.164
  21.5 0.1 copy.7
  21.7 0.9 convolution_convert_fusion.3
  22.6 0.0 all-reduce.4.cloned.1.call-update
  22.6 0.0 all-reduce.6.cloned.1.call-start
  22.7 0.2 select_reduce_fusion.2
  22.9 1.3 iota_subtract_fusion
  24.2 0.2 select_reduce_fusion.1
  24.4 0.0 copy-start.4
  24.4 3.8 %fusion.6 = bf16[128,512]{1,0:T(8,128)(2,1)S(1)} fusion(bf16[512,4096]{1,0:T(8,128)(2,1)} %param.3, s32[128]{0:T(128)S(1)} %broadcast_add_fusion.1), kind=kOutput, calls=%fused_computation.17 | convolution fusion | flops 537460736 | bytes 4325888 | tf_op jit(solution)/shard_map/dot_general | solution.py:33
  28.3 0.0 copy-done.4
  28.3 1.5 fusion.4
  29.8 84.5 %all-reduce.4.cloned.1.call-done = bf16[256,512]{1,0:T(8,128)(2,1)} async-done(((bf16[256,512]{1,0:T(8,128)(2,1)}), bf16[256,512]{1,0:T(8,128)(2,1)}) %all-reduce.4.cloned.1.call-update) | async-done | bytes 262160 | tf_op jit(solution)/shard_map/psum | solution.py:53
  114.3 1.2 convolution_convert_fusion.5
  115.5 5.1 %all-gather.1 = bf16[512,128]{1,0:T(8,128)(2,1)S(1)} all-gather(bf16[256,128]{1,0:T(8,128)(2,1)S(1)} %convolution_convert_fusion.5), channel_id=3, replica_groups=mesh['row'=2,'col'=16] {'row'}, dimensions={0}, use_global_device_ids=true | all-gather | bytes 196608 | tf_op jit(solution)/shard_map/all_gather | solution.py:45
  120.6 0.3 convolution_add_fusion.2
  120.9 0.9 convolution_convert_fusion.2
  121.8 0.0 all-reduce.6.cloned.1.call-update
  121.8 0.0 all-reduce.8.cloned.1.call-start
  121.9 90.2 %all-reduce.6.cloned.1.call-done = bf16[256,512]{1,0:T(8,128)(2,1)} async-done(((bf16[256,512]{1,0:T(8,128)(2,1)}), bf16[256,512]{1,0:T(8,128)(2,1)}) %all-reduce.6.cloned.1.call-update) | async-done | bytes 262160 | tf_op jit(solution)/shard_map/psum | solution.py:53
  212.1 1.2 convolution_convert_fusion.4
  213.2 5.1 %all-gather.2 = bf16[512,128]{1,0:T(8,128)(2,1)S(1)} all-gather(bf16[256,128]{1,0:T(8,128)(2,1)S(1)} %convolution_convert_fusion.4), channel_id=4, replica_groups=mesh['row'=2,'col'=16] {'row'}, dimensions={0}, use_global_device_ids=true | all-gather | bytes 196608 | tf_op jit(solution)/shard_map/all_gather | solution.py:45
  218.4 0.3 convolution_add_fusion.1
  218.7 0.9 convolution_convert_fusion.1
  219.6 0.0 all-reduce.8.cloned.1.call-update
  219.6 0.0 reduce-scatter.2.cloned.1.call-start
  219.6 90.2 %all-reduce.8.cloned.1.call-done = bf16[256,512]{1,0:T(8,128)(2,1)} async-done(((bf16[256,512]{1,0:T(8,128)(2,1)}), bf16[256,512]{1,0:T(8,128)(2,1)}) %all-reduce.8.cloned.1.call-update) | async-done | bytes 262160 | tf_op jit(solution)/shard_map/psum | solution.py:53
  309.8 4.9 %convolution_convert_fusion = bf16[256,4096]{1,0:T(8,128)(2,1)} fusion(bf16[512,4096]{1,0:T(8,128)(2,1)} %param.3, f32[256,512]{1,0:T(8,128)S(1)} %copy-done, bf16[256,512]{1,0:T(8,128)(2,1)} %all-reduce.8.cloned.1.call-done), kind=kOutput, calls=%fused_computation | convolution fusion | flops 1075183616 | bytes 7077888 | tf_op jit(solution)/shard_map/dot_general | solution.py:55
  314.7 0.0 copy-start.1
  314.7 0.0 copy-start.2
  314.7 0.0 copy-start.3
  314.7 0.0 reduce-scatter.2.cloned.1.call-update
  314.7 0.2 select_reduce_fusion
  314.9 0.3 convert_reduce_fusion
  315.3 0.4 copy-done.1
  315.7 0.1 copy-done.2
  315.7 0.1 copy-done.3
  315.8 1.0 multiply_reduce_fusion.1
  316.8 30.5 %reduce-scatter.2.cloned.1.call-done = bf16[128,4096]{1,0:T(8,128)(2,1)} async-done(((bf16[256,4096]{1,0:T(8,128)(2,1)}), bf16[128,4096]{1,0:T(8,128)(2,1)}) %reduce-scatter.2.cloned.1.call-update) | async-done | bytes 1048592 | tf_op jit(solution)/shard_map/reduce_scatter | solution.py:54
  347.3 4.1 %multiply_reduce_fusion = (f32[4096]{0:T(1024)S(1)}, f32[128,4096]{1,0:T(8,128)}) fusion(f32[4096]{0:T(1024)S(1)} %convert_reduce_fusion, bf16[128,4096]{1,0:T(8,128)(2,1)} %reduce-scatter.2.cloned.1.call-done, s32[128]{0:T(128)S(1)} %broadcast_add_fusion.1, f32[256,128]{1,0:T(8,128)S(1)} %convolution_add_fusion.1, s32[]{:T(128)S(6)} %select_n.19), kind=kOutput, calls=%fused_computation.2 | convolution fusion | flops 808972288 | bytes 3244548 | tf_op jit(solution)/shard_map/dot_general | solution.py:61
  351.4 2.6 concatenate.3
  354.0 7.1 %psum.31 = f32[4100]{0:T(1024)S(1)} all-reduce(f32[4100]{0:T(1024)S(1)} %concatenate.3), channel_id=1, replica_groups=mesh['row'=2,'col'=16] {'row'}, use_global_device_ids=true, to_apply=%region_21.22 | all-reduce | flops 4100 | bytes 32800 | tf_op jit(solution)/shard_map/psum | solution.py:64
  361.1 0.5 slice_multiply_fusion
  361.6 0.6 slice_sqrt_fusion
  (9 shorter events, 0.1 us)
Async XLA Ops:
  7.2 107.1 %all-reduce.4.cloned.1.call-start = ((), (), s32[]{:S(2)}) async-start(), calls=%async_computation.1 | async-start | bytes 524288 | tf_op jit(solution)/shard_map/psum | solution.py:53
  11.3 3.8 %copy-start = (f32[256,512]{1,0:T(8,128)S(1)}, f32[256,512]{1,0:T(8,128)}, u32[]{:S(2)}) copy-start(f32[256,512]{1,0:T(8,128)} %param.4) | copy-start | bytes 1572868
  22.6 189.5 %all-reduce.6.cloned.1.call-start = ((), (), s32[]{:S(2)}) async-start(), calls=%async_computation.2 | async-start | bytes 524288 | tf_op jit(solution)/shard_map/psum | solution.py:53
  24.4 3.9 %copy-start.4 = (bf16[512,4096]{1,0:T(8,128)(2,1)S(1)}, bf16[512,4096]{1,0:T(8,128)(2,1)}, u32[]{:S(2)}) copy-start(bf16[512,4096]{1,0:T(8,128)(2,1)} %param.3) | copy-start | bytes 12582916
  121.8 188.0 %all-reduce.8.cloned.1.call-start = ((), (), s32[]{:S(2)}) async-start(), calls=%async_computation.3 | async-start | bytes 524288 | tf_op jit(solution)/shard_map/psum | solution.py:53
  219.6 127.7 %reduce-scatter.2.cloned.1.call-start = ((), (), s32[]{:S(2)}) async-start(), calls=%async_computation.4 | async-start | bytes 3145728 | tf_op jit(solution)/shard_map/reduce_scatter | solution.py:54
  314.7 0.9 copy-start.1
  314.7 1.0 copy-start.2
  314.7 1.1 copy-start.3
Sparse Core Ops, SparseCore 0:
  22.7 91.5 all-reduce.3
  122.0 90.0 all-reduce.5
  219.7 90.0 all-reduce.7
  314.9 32.3 reduce-scatter.1
